TPU v7x, 32 devices: a whole 2x2x4 slice. The times are simulated.
32 devices in a mesh: sec: 2 (over y), tp: 4 (over x, core), dp: 4 (over z).
Axes of the slice: x: 2, y: 2, z: 4, core: 2. Of those that a mesh axis runs over, the one named last changes fastest.
Arguments:
- feats: bfloat16 [8, 512, 512], P(('sec', 'dp'), 'tp'), may hold values from -6 to 6
- frame_clip: int32 [8, 32], P(('sec', 'dp')), may hold values from 0 to 3, never falling along the last dimension, each value on 1 to 16 neighbouring positions
- clip_order: int32 [8, 4], P(('sec', 'dp')), may hold values from 0 to 3, each once within a row
- conv_weight: bfloat16 [3, 512, 192], replicated, may hold values from -0.15625 to 0.15625
- embed_weight: bfloat16 [192, 3072], replicated, may hold values from -0.4375 to 0.4375
- wq: bfloat16 [3072, 512], P(('sec', 'dp'), 'tp')
- wk: bfloat16 [3072, 512], P(('sec', 'dp'), 'tp')
- wv: bfloat16 [3072, 512], P(('sec', 'dp'), 'tp'), may hold values from -0.109375 to 0.109375
- q_gain: float32 [4, 128], P('tp'), may hold values from 0.6 to 8, as said below
- k_gain: float32 [4, 128], P('tp'), may hold values from 0.6 to 8, as said below
Outputs:
- attended: bfloat16 [8, 512, 512], P(('sec', 'dp'), 'tp')
Inputs may be any that keep to these rules, and one draw needn't show every extreme that they name: `frame_clip`: clip ids never fall along the frames; every clip has at least one frame and one clip has exactly 16 frames. `clip_order`: each row holds every clip once. `q_gain`: positive. `k_gain`: positive.
All inputs are finite; a program needn't handle non-finite values.
Results may differ from a plain program's by a relative error of at most 0.0084.
Values may be sent and summed in bfloat16 or wider, within the bound.
A program may use at most 64 MiB of HBM per device.

v0:
```python
import jax
import jax.numpy as jnp
from jax import lax
from jax.sharding import PartitionSpec as P

HD = 128
PD = 192
TAPS = 3
VP = 16


def from_behind(value, axis, steps):
    count = lax.axis_size(axis)
    leading, last = (max(0, -steps), min(count, count - steps))
    return lax.ppermute(value, axis, [(source, source + steps) for source in range(leading, last)])


def packing(clip_ids, clip_order):
    frame_count = clip_ids.shape[0]
    clip_count = clip_order.shape[0]
    labels = jnp.arange(clip_count, dtype=jnp.int32)
    lengths = jnp.sum((clip_ids[None, :] == labels[:, None]).astype(jnp.int32), axis=1)
    starts = jnp.cumsum(lengths) - lengths
    picked = clip_order[:, None] == labels[None, :]
    packed_len = jnp.sum(jnp.where(picked, lengths[None, :], 0), axis=1)
    packed_from = jnp.sum(jnp.where(picked, starts[None, :], 0), axis=1)
    place_start = jnp.cumsum(packed_len) - packed_len
    frames = jnp.arange(frame_count, dtype=jnp.int32)
    places = jnp.sum((frames[:, None] >= place_start[None, :]).astype(jnp.int32), axis=1) - 1
    chosen = places[:, None] == labels[None, :]
    source = jnp.sum(jnp.where(chosen, (packed_from - place_start)[None, :], 0), axis=1) + frames
    return (source, places)


def normed(values, gains):
    scale = lax.rsqrt(jnp.mean(values * values, axis=-1, keepdims=True) + 1e-06)
    return (values * scale * gains[None, :]).astype(jnp.bfloat16)


def attend_local(projected, slots, segment, gain_q, gain_k):
    ordered = jnp.take(projected, slots, axis=0)
    query = normed(ordered[:, :HD], gain_q)
    key_rows = normed(ordered[:, HD : 2 * HD], gain_k)
    value_rows = ordered[:, 2 * HD :].astype(jnp.bfloat16)
    total = query.shape[0]
    block = min(total, 512)
    query_blocks = query.reshape(total // block, block, HD)
    segment_blocks = segment.reshape(total // block, block)

    def one_block(inputs):
        query_rows, block_seg = inputs
        scores = jnp.dot(query_rows, key_rows.T, preferred_element_type=jnp.float32) * HD ** (-0.5)
        same_seg = block_seg[:, None] == segment[None, :]
        scores = jnp.where(same_seg, scores, -1e30)
        highest = jnp.max(scores, axis=-1, keepdims=True)
        expo = jnp.where(same_seg, jnp.exp(scores - highest), 0.0)
        probs = (expo / jnp.sum(expo, axis=-1, keepdims=True)).astype(jnp.bfloat16)
        return jnp.dot(probs, value_rows, preferred_element_type=jnp.float32).astype(jnp.bfloat16)

    mixed = lax.map(one_block, (query_blocks, segment_blocks))
    return mixed.reshape(total, HD)


def embed_project(every_latent, embed_weight, w_qkv):
    all_tokens = jnp.dot(every_latent, embed_weight, preferred_element_type=jnp.float32).astype(
        jnp.bfloat16
    )
    return jnp.dot(all_tokens, w_qkv, preferred_element_type=jnp.float32)


def local(feats, frame_clip, clip_order, conv_weight, embed_weight, wq, wk, wv, q_gain, k_gain):
    feature = feats[0]
    row_count = feature.shape[0]
    frames_dev = row_count // VP
    reach = TAPS - 1
    rim_rows = from_behind(feature[row_count - reach * VP :], "tp", 1)
    widened = jnp.concatenate([rim_rows, feature], axis=0)
    clip_ids = frame_clip[0]
    padded = jnp.concatenate([jnp.full((reach,), -1, jnp.int32), clip_ids])
    window = lax.dynamic_slice_in_dim(padded, lax.axis_index("tp") * frames_dev, frames_dev + reach)
    own_ids = window[reach:]
    summed = jnp.zeros((row_count, PD), jnp.float32)
    for delay in range(TAPS):
        first = reach - delay
        earlier = widened[first * VP : (first + frames_dev) * VP]
        in_clip = jnp.repeat(window[first : first + frames_dev] == own_ids, VP)
        contrib = jnp.dot(earlier, conv_weight[delay], preferred_element_type=jnp.float32)
        summed = summed + jnp.where(in_clip[:, None], contrib, 0.0)
    latent = summed.astype(jnp.bfloat16)
    full_q, full_k, full_v = (
        lax.all_gather(wq, ("sec", "dp"), axis=0, tiled=True),
        lax.all_gather(wk, ("sec", "dp"), axis=0, tiled=True),
        lax.all_gather(wv, ("sec", "dp"), axis=0, tiled=True),
    )
    w_qkv = jnp.concatenate([full_q, full_k, full_v], axis=1)
    source, places = packing(clip_ids, clip_order[0])
    slots = (source[:, None] * VP + jnp.arange(VP, dtype=jnp.int32)[None, :]).reshape(-1)
    segment = jnp.repeat(places, VP)
    flat_latent = latent.reshape(row_count * PD // 128, 128)
    every_latent = lax.all_gather(flat_latent, "tp", axis=0, tiled=True).reshape(-1, PD)
    projected = embed_project(every_latent, embed_weight, w_qkv)
    mixed = attend_local(projected, slots, segment, q_gain[0], k_gain[0])
    regrouped = lax.all_to_all(mixed, "tp", split_axis=0, concat_axis=1, tiled=True)
    return regrouped[None]


def solution(mesh):
    return jax.shard_map(
        local,
        mesh=mesh,
        in_specs=(
            P(("sec", "dp"), "tp", None),
            P(("sec", "dp"), None),
            P(("sec", "dp"), None),
            P(),
            P(),
            P(("sec", "dp"), "tp"),
            P(("sec", "dp"), "tp"),
            P(("sec", "dp"), "tp"),
            P("tp", None),
            P("tp", None),
        ),
        out_specs=P(("sec", "dp"), "tp", None),
        check_vma=False,
    )
```

profile of v0, /device:TPU:0, one launch (start us, length us, event | category | flops | bytes accessed | tf_op | source)
XLA Modules:
  0.0 136.3 jit_solution(9821429094563022714)
XLA Ops:
  0.0 0.0 copy-start
  0.0 0.0 copy-start.2
  0.0 0.9 slice_bitcast_fusion
  0.9 2.4 %collective-permute-start = (bf16[32,512]{1,0:T(8,128)(2,1)S(1)}, bf16[32,512]{1,0:T(8,128)(2,1)S(1)}, u32[]{:S(2)}, u32[]{:S(2)}) collective-permute-start(bf16[32,512]{1,0:T(8,128)(2,1)S(1)} %slice_bitcast_fusion), channel_id=1, source_target_pairs={{0,4},{4,8},{8,12},{1,5},{5,9},{9,13},{2,6},{6,10},{10,14},{3,7},{... | collective-permute-start | bytes 98312 | tf_op jit(solution)/shard_map/ppermute | solution.py:15
  3.3 0.8 convert_reduce_fusion.1
  4.0 0.2 reduce-window.16
  4.2 0.9 select_reduce_fusion.1
  5.1 0.2 reduce-window.15
  5.3 0.1 convert_reduce_fusion
  5.4 0.1 select_reduce_fusion
  5.5 0.1 iota_add_fusion
  5.5 0.1 add.101
  5.6 0.1 add.95
  5.7 0.0 copy-start.1
  5.7 34.9 %all_gather.15 = bf16[3072,128]{1,0:T(8,128)(2,1)S(1)} all-gather(bf16[384,128]{1,0:T(8,128)(2,1)} %param.17), channel_id=1, replica_groups=mesh['sec'=2,'tp'=4,'dp'=4] {'sec','dp'}, dimensions={0}, use_global_device_ids=true | all-gather | bytes 884736 | tf_op jit(solution)/shard_map/all_gather | solution.py:93
  40.6 0.0 copy-start.3
  40.6 34.3 %all_gather.14 = bf16[3072,128]{1,0:T(8,128)(2,1)S(1)} all-gather(bf16[384,128]{1,0:T(8,128)(2,1)} %param.16), channel_id=1, replica_groups=mesh['sec'=2,'tp'=4,'dp'=4] {'sec','dp'}, dimensions={0}, use_global_device_ids=true | all-gather | bytes 884736 | tf_op jit(solution)/shard_map/all_gather | solution.py:92
  75.0 0.0 copy-done.2
  75.0 35.1 %all_gather.13 = bf16[3072,128]{1,0:T(8,128)(2,1)} all-gather(bf16[384,128]{1,0:T(8,128)(2,1)S(1)} %copy-done.2), channel_id=1, replica_groups=mesh['sec'=2,'tp'=4,'dp'=4] {'sec','dp'}, dimensions={0}, use_global_device_ids=true | all-gather | bytes 884736 | tf_op jit(solution)/shard_map/all_gather | solution.py:91
  110.0 0.0 copy-done.1
  110.0 1.1 fusion.13
  111.2 0.0 copy-done.3
  111.2 0.1 pad_dynamic-slice_fusion
  111.3 0.1 slice_compare_fusion
  111.4 0.1 broadcast_in_dim.118
  111.5 0.1 broadcast_in_dim.119
  111.6 0.1 broadcast_in_dim.122
  111.6 0.1 broadcast_in_dim.123
  111.7 0.1 broadcast_in_dim.113
  111.8 0.1 eq.80
  111.9 0.0 collective-permute-done
  111.9 1.1 fusion.8
  113.0 1.1 fusion.9
  114.2 0.1 copy.14
  114.3 0.1 reshape.156
  114.4 5.6 %all_gather.12 = bf16[768,128]{1,0:T(8,128)(2,1)S(1)} all-gather(bf16[192,128]{1,0:T(8,128)(2,1)S(1)} %reshape.156), channel_id=1, replica_groups=mesh['sec'=2,'tp'=4,'dp'=4] {'tp'}, dimensions={0}, use_global_device_ids=true | all-gather | bytes 245760 | tf_op jit(solution)/shard_map/all_gather | solution.py:100
  120.0 0.9 reshape.157
  120.9 0.0 copy-done
  120.9 3.8 %fusion = f32[512,384]{1,0:T(8,128)S(1)} fusion(bf16[3072,128]{1,0:T(8,128)(2,1)S(1)} %all_gather.15, bf16[3072,128]{1,0:T(8,128)(2,1)S(1)} %all_gather.14, bf16[3072,128]{1,0:T(8,128)(2,1)} %all_gather.13, bf16[512,192]{1,0:T(8,128)(2,1)} %reshape.157, bf16[192,3072]{1,0:T(8,128)(2,1)S(1)} %copy-done), kind=kOutput, calls=%fused_computation.2 | convolution fusion | flops 1820590080 | bytes 4521984 | tf_op jit(solution)/shard_map/dot_general | solution.py:68
  124.7 1.6 %gather_fusion = f32[512,384]{1,0:T(8,128)S(1)} fusion(f32[512,384]{1,0:T(8,128)S(1)} %fusion, s32[1024]{0:T(1024)S(1)} %pad_clamp_fusion), kind=kCustom, calls=%fused_computation | custom fusion | bytes 1574912 | tf_op jit(solution)/shard_map/jit(_take)/gather | solution.py:41
  126.3 0.0 copy-start.4
  126.4 0.0 copy-start.5
  126.4 0.1 broadcast_select_fusion
  126.5 0.2 multiply_reduce_fusion.1
  126.7 0.3 copy-done.4
  127.0 0.0 copy-done.5
  127.0 0.4 fusion.31
  127.5 0.2 fusion.10
  127.7 0.5 convolution_convert_fusion.1
  128.2 7.3 %all_to_all.16 = bf16[4,128,128]{2,1,0:T(8,128)(2,1)S(1)} all-to-all(bf16[4,128,128]{2,1,0:T(8,128)(2,1)S(1)} %bitcast.33), channel_id=1, replica_groups=mesh['sec'=2,'tp'=4,'dp'=4] {'tp'}, dimensions={0} | all-to-all | bytes 262144 | tf_op jit(solution)/shard_map/all_to_all | solution.py:103
  135.5 0.1 copy.15
  135.6 0.7 broadcast_in_dim.128
  (8 shorter events, 0.1 us)
Async XLA Ops:
  0.0 120.9 %copy-start = (bf16[192,3072]{1,0:T(8,128)(2,1)S(1)}, bf16[192,3072]{1,0:T(8,128)(2,1)}, u32[]{:S(2)}) copy-start(bf16[192,3072]{1,0:T(8,128)(2,1)} %param.14) | copy-start | bytes 3538948
  0.0 75.0 %copy-start.2 = (bf16[384,128]{1,0:T(8,128)(2,1)S(1)}, bf16[384,128]{1,0:T(8,128)(2,1)}, u32[]{:S(2)}) copy-start(bf16[384,128]{1,0:T(8,128)(2,1)} %param.15) | copy-start | bytes 294916
  0.9 111.0 %collective-permute-start = (bf16[32,512]{1,0:T(8,128)(2,1)S(1)}, bf16[32,512]{1,0:T(8,128)(2,1)S(1)}, u32[]{:S(2)}, u32[]{:S(2)}) collective-permute-start(bf16[32,512]{1,0:T(8,128)(2,1)S(1)} %slice_bitcast_fusion), channel_id=1, source_target_pairs={{0,4},{4,8},{8,12},{1,5},{5,9},{9,13},{2,6},{6,10},{10,14},{3,7},{... | collective-permute-start | bytes 98312 | tf_op jit(solution)/shard_map/ppermute | solution.py:15
  5.7 104.3 %copy-start.1 = (bf16[1,128,512]{2,1,0:T(8,128)(2,1)S(1)}, bf16[1,128,512]{2,1,0:T(8,128)(2,1)}, u32[]{:S(2)}) copy-start(bf16[1,128,512]{2,1,0:T(8,128)(2,1)} %param.10) | copy-start | bytes 393220
  40.6 70.6 %copy-start.3 = (s32[1,32]{1,0:T(1,128)S(1)}, s32[1,32]{1,0:T(1,128)}, u32[]{:S(2)}) copy-start(s32[1,32]{1,0:T(1,128)} %param.11) | copy-start | bytes 388
  126.3 0.7 copy-start.4
  126.4 0.7 copy-start.5
where the time goes:
time: 137 us; the launch traced here: 136 us
  blocking collectives  117 us (85%)
  matrix products  8.16 us (6%)
  local copies, waits for them, and re-layouts  5.43 us (4%)
  other arithmetic  2.97 us (2%)
  starting transfers between devices  2.39 us (2%)
    all_gather x1, blocking collectives, local(): lax.all_gather(wq, ('sec', 'dp'), axis=0, tiled=True)  35.1 us
    all_gather x1, blocking collectives, local(): lax.all_gather(wv, ('sec', 'dp'), axis=0, tiled=True)  34.9 us
    all_gather x1, blocking collectives, local(): lax.all_gather(wk, ('sec', 'dp'), axis=0, tiled=True)  34.3 us
    all_to_all x1, blocking collectives, local(): lax.all_to_all(mixed, 'tp', split_axis=0, concat_axis=1, tiled=True)  7.29 us
    all_gather x1, blocking collectives, local(): lax.all_gather(flat_latent, 'tp', axis=0, tiled=True).reshape(-1, PD)  5.6 us
    dot_general x1, matrix products, embed_project(): return jnp.dot(all_tokens, w_qkv, preferred_element_type=jnp.float32)  3.81 us
    dot_general x3, matrix products, local(): jnp.dot(earlier, conv_weight[delay], preferred_element_type=jnp.float32)  3.42 us
  transfers between devices with their start and end apart: 1, of which 0 were waited for; matrix products, arithmetic and copies ran while one was open for 3% of the time, Pallas kernels for 0%

commit v1 on v0

--- a/solution.py
+++ b/solution.py
@@ -7,6 +7,27 @@
 PD = 192
 TAPS = 3
 VP = 16
+
+
+def collect(array, axis, dim):
+    size, position, extent = (lax.axis_size(axis), lax.axis_index(axis), array.shape[dim])
+    right = [(i, (i + 1) % size) for i in range(size)]
+    behind = [(i, (i - 1) % size) for i in range(size)]
+    out = jnp.zeros((*array.shape[:dim], size * extent, *array.shape[dim + 1 :]), array.dtype)
+    out = lax.dynamic_update_slice_in_dim(out, array, position * extent, axis=dim)
+    from_left = from_right = array
+    half = size // 2
+    for hop in range(1, half + 1):
+        from_left = lax.ppermute(from_left, axis, right)
+        out = lax.dynamic_update_slice_in_dim(
+            out, from_left, (position - hop) % size * extent, axis=dim
+        )
+        if hop < size - half:
+            from_right = lax.ppermute(from_right, axis, behind)
+            out = lax.dynamic_update_slice_in_dim(
+                out, from_right, (position + hop) % size * extent, axis=dim
+            )
+    return out
 
 
 def from_behind(value, axis, steps):
@@ -89,7 +110,7 @@
     latent = summed.astype(jnp.bfloat16)
     full_q, full_k, full_v = (
         lax.all_gather(wq, ("sec", "dp"), axis=0, tiled=True),
-        lax.all_gather(wk, ("sec", "dp"), axis=0, tiled=True),
+        collect(wk, ("sec", "dp"), 0),
         lax.all_gather(wv, ("sec", "dp"), axis=0, tiled=True),
     )
     w_qkv = jnp.concatenate([full_q, full_k, full_v], axis=1)

time: 137 us -> 132 us (0.964)
  blocking collectives: 117 us -> 81.3 us
  starting transfers between devices: 2.39 us -> 17 us
  waiting for transfers between devices: 0.01 us -> 9.79 us
  local copies, waits for them, and re-layouts: 5.43 us -> 12.1 us
    all_gather x1 -> x0, blocking collectives: 34.3 us -> none  [local(): lax.all_gather(wk, ('sec', 'dp'), axis=0, tiled=True)]
    ppermute x0 -> x7, starting transfers between devices: none -> 15.5 us  [the longest x3 12.5 us: collect(): from_right = lax.ppermute(from_right, axis, behind)]
    ppermute x0 -> x7, waiting for transfers between devices: none -> 9.79 us  [the longest x4 9.78 us: collect(): from_left = lax.ppermute(from_left, axis, right)]
    dynamic_update_slice x0 -> x8, local copies, waits for them, and re-layouts: none -> 5.11 us  [the longest x4 2.55 us: collect(): lax.dynamic_update_slice_in_dim(out, from_left, (position - hop) % size *...]
    all_gather x1, blocking collectives: 34.9 us -> 33.2 us  [local(): lax.all_gather(wv, ('sec', 'dp'), axis=0, tiled=True)]
  transfers between devices with their start and end apart: 1 -> 8, of which waited for: 0 -> 3; matrix products, arithmetic and copies ran while one was open for 3% -> 11% of each run, Pallas kernels for 0% -> 0%
where the time goes in v1:
time: 132 us; the launch traced here: 131 us
  blocking collectives  81.3 us (62%)
  starting transfers between devices  17 us (13%)
  local copies, waits for them, and re-layouts  12.1 us (9%)
  waiting for transfers between devices  9.79 us (7%)
  matrix products  8.21 us (6%)
  other arithmetic  2.97 us (2%)
    all_gather x1, blocking collectives, local(): lax.all_gather(wq, ('sec', 'dp'), axis=0, tiled=True)  34.2 us
    all_gather x1, blocking collectives, local(): lax.all_gather(wv, ('sec', 'dp'), axis=0, tiled=True)  33.2 us
    ppermute x3, starting transfers between devices, collect(): from_right = lax.ppermute(from_right, axis, behind)  12.5 us
    ppermute x4, waiting for transfers between devices, collect(): from_left = lax.ppermute(from_left, axis, right)  9.78 us
    all_to_all x1, blocking collectives, local(): lax.all_to_all(mixed, 'tp', split_axis=0, concat_axis=1, tiled=True)  7.37 us
    all_gather x1, blocking collectives, local(): lax.all_gather(flat_latent, 'tp', axis=0, tiled=True).reshape(-1, PD)  6.46 us
    dot_general x1, matrix products, embed_project(): return jnp.dot(all_tokens, w_qkv, preferred_element_type=jnp.float32)  3.81 us
    dot_general x3, matrix products, local(): jnp.dot(earlier, conv_weight[delay], preferred_element_type=jnp.float32)  3.47 us
  transfers between devices with their start and end apart: 8, of which 3 were waited for; matrix products, arithmetic and copies ran while one was open for 11% of the time, Pallas kernels for 0%

profile of v1, /device:TPU:0, one launch (start us, length us, event | category | flops | bytes accessed | tf_op | source)
XLA Modules:
  0.0 131.5 jit_solution(10138315781990284085)
XLA Ops:
  0.0 3.1 %collective-permute-start.1 = (bf16[384,128]{1,0:T(8,128)(2,1)}, bf16[384,128]{1,0:T(8,128)(2,1)S(1)}, u32[]{:S(2)}, u32[]{:S(2)}) collective-permute-start(bf16[384,128]{1,0:T(8,128)(2,1)} %param.16), channel_id=1, source_target_pairs={{0,1},{1,2},{2,3},{3,16},{16,17},{17,18},{18,19},{19,0},{4,5},{5,6... | collective-permute-start | bytes 294920 | tf_op jit(solution)/shard_map/ppermute | solution.py:21
  3.1 3.0 %collective-permute-start.2 = (bf16[384,128]{1,0:T(8,128)(2,1)}, bf16[384,128]{1,0:T(8,128)(2,1)S(1)}, u32[]{:S(2)}, u32[]{:S(2)}) collective-permute-start(bf16[384,128]{1,0:T(8,128)(2,1)} %param.16), channel_id=1, source_target_pairs={{0,19},{1,0},{2,1},{3,2},{16,3},{17,16},{18,17},{19,18},{4,23},{5,... | collective-permute-start | bytes 294920 | tf_op jit(solution)/shard_map/ppermute | solution.py:26
  6.1 0.8 slice_bitcast_fusion
  6.9 1.4 %collective-permute-start = (bf16[32,512]{1,0:T(8,128)(2,1)S(1)}, bf16[32,512]{1,0:T(8,128)(2,1)S(1)}, u32[]{:S(2)}, u32[]{:S(2)}) collective-permute-start(bf16[32,512]{1,0:T(8,128)(2,1)S(1)} %slice_bitcast_fusion), channel_id=1, source_target_pairs={{0,4},{4,8},{8,12},{1,5},{5,9},{9,13},{2,6},{6,10},{10,14},{3,7},{... | collective-permute-start | bytes 98312 | tf_op jit(solution)/shard_map/ppermute | solution.py:36
  8.3 0.8 convert_reduce_fusion.1
  9.1 0.2 reduce-window.16
  9.3 0.9 select_reduce_fusion.1
  10.2 0.2 reduce-window.15
  10.3 0.1 convert_reduce_fusion
  10.4 0.1 select_reduce_fusion
  10.5 0.1 iota_add_fusion
  10.6 0.1 add.182
  10.7 0.1 add.157
  10.8 0.7 pad_dynamic-slice_fusion
  11.5 0.1 slice_compare_fusion
  11.6 1.2 fusion.13
  12.8 0.0 copy-start.3
  12.8 34.2 %all_gather.10 = bf16[3072,128]{1,0:T(8,128)(2,1)S(1)} all-gather(bf16[384,128]{1,0:T(8,128)(2,1)} %param.15), channel_id=1, replica_groups=mesh['sec'=2,'tp'=4,'dp'=4] {'sec','dp'}, dimensions={0}, use_global_device_ids=true | all-gather | bytes 884736 | tf_op jit(solution)/shard_map/all_gather | solution.py:112
  47.0 33.2 %all_gather.11 = bf16[3072,128]{1,0:T(8,128)(2,1)S(1)} all-gather(bf16[384,128]{1,0:T(8,128)(2,1)S(1)} %copy-done.2), channel_id=1, replica_groups=mesh['sec'=2,'tp'=4,'dp'=4] {'sec','dp'}, dimensions={0}, use_global_device_ids=true | all-gather | bytes 884736 | tf_op jit(solution)/shard_map/all_gather | solution.py:114
  80.3 1.0 broadcast_in_dim.128
  81.3 0.6 constant_dynamic-update-slice_fusion.7
  81.9 0.1 broadcast_in_dim.121
  82.0 0.1 broadcast_in_dim.122
  82.1 0.1 broadcast_in_dim.125
  82.1 0.1 broadcast_in_dim.126
  82.2 0.1 broadcast_in_dim.116
  82.3 0.1 eq.88
  82.4 0.0 collective-permute-done
  82.4 1.1 fusion.8
  83.5 1.1 fusion.9
  84.7 0.1 copy.14
  84.8 0.1 reshape.156
  84.9 6.5 %all_gather.9 = bf16[768,128]{1,0:T(8,128)(2,1)S(1)} all-gather(bf16[192,128]{1,0:T(8,128)(2,1)S(1)} %reshape.156), channel_id=1, replica_groups=mesh['sec'=2,'tp'=4,'dp'=4] {'tp'}, dimensions={0}, use_global_device_ids=true | all-gather | bytes 245760 | tf_op jit(solution)/shard_map/all_gather | solution.py:121
  91.4 0.9 reshape.157
  92.3 0.0 collective-permute-done.1
  92.3 0.0 collective-permute-start.3
  92.3 0.0 collective-permute-done.2
  92.3 4.7 %collective-permute-start.4 = (bf16[384,128]{1,0:T(8,128)(2,1)S(1)}, bf16[384,128]{1,0:T(8,128)(2,1)S(1)}, u32[]{:S(2)}, u32[]{:S(2)}) collective-permute-start(bf16[384,128]{1,0:T(8,128)(2,1)S(1)} %collective-permute-done.2), channel_id=1, source_target_pairs={{0,19},{1,0},{2,1},{3,2},{16,3},{17,16},{18,17},{19,18},{4,23},{5,... | collective-permute-start | bytes 294920 | tf_op jit(solution)/shard_map/ppermute | solution.py:26
  97.0 0.6 constant_dynamic-update-slice_fusion.6
  97.7 0.6 constant_dynamic-update-slice_fusion.5
  98.3 2.4 %collective-permute-done.3 = bf16[384,128]{1,0:T(8,128)(2,1)S(1)} collective-permute-done((bf16[384,128]{1,0:T(8,128)(2,1)S(1)}, bf16[384,128]{1,0:T(8,128)(2,1)S(1)}, u32[]{:S(2)}, u32[]{:S(2)}) %collective-permute-start.3) | collective-permute-done | bytes 98336 | tf_op jit(solution)/shard_map/ppermute | solution.py:21
  100.7 0.0 collective-permute-start.5
  100.7 4.7 %collective-permute-start.6 = (bf16[384,128]{1,0:T(8,128)(2,1)S(1)}, bf16[384,128]{1,0:T(8,128)(2,1)S(1)}, u32[]{:S(2)}, u32[]{:S(2)}) collective-permute-start(bf16[384,128]{1,0:T(8,128)(2,1)S(1)} %collective-permute-done.4), channel_id=1, source_target_pairs={{0,19},{1,0},{2,1},{3,2},{16,3},{17,16},{18,17},{19,18},{4,23},{5,... | collective-permute-start | bytes 294920 | tf_op jit(solution)/shard_map/ppermute | solution.py:26
  105.4 0.6 constant_dynamic-update-slice_fusion.4
  106.1 0.6 constant_dynamic-update-slice_fusion.3
  106.7 1.4 %collective-permute-done.5 = bf16[384,128]{1,0:T(8,128)(2,1)S(1)} collective-permute-done((bf16[384,128]{1,0:T(8,128)(2,1)S(1)}, bf16[384,128]{1,0:T(8,128)(2,1)S(1)}, u32[]{:S(2)}, u32[]{:S(2)}) %collective-permute-start.5) | collective-permute-done | bytes 98336 | tf_op jit(solution)/shard_map/ppermute | solution.py:21
  108.1 0.6 constant_dynamic-update-slice_fusion.2
  108.7 0.7 constant_dynamic-update-slice_fusion.1
  109.4 6.0 %collective-permute-done.7 = bf16[384,128]{1,0:T(8,128)(2,1)S(1)} collective-permute-done((bf16[384,128]{1,0:T(8,128)(2,1)S(1)}, bf16[384,128]{1,0:T(8,128)(2,1)S(1)}, u32[]{:S(2)}, u32[]{:S(2)}) %collective-permute-start.7) | collective-permute-done | bytes 98336 | tf_op jit(solution)/shard_map/ppermute | solution.py:21
  115.4 0.6 constant_dynamic-update-slice_fusion
  116.0 3.8 %fusion = f32[512,384]{1,0:T(8,128)S(1)} fusion(bf16[3072,128]{1,0:T(8,128)(2,1)S(1)} %all_gather.11, bf16[3072,128]{1,0:T(8,128)(2,1)} %constant_dynamic-update-slice_fusion, bf16[3072,128]{1,0:T(8,128)(2,1)S(1)} %all_gather.10, bf16[512,192]{1,0:T(8,128)(2,1)} %reshape.157, bf16[192,3072]{1,0:T(8,128)(2,1)S(1)} %copy-done), kind=kOutput, calls=%fused_computation.2 | convolution fusion | flops 1820590080 | bytes 4521984 | tf_op jit(solution)/shard_map/dot_general | solution.py:89
  119.8 1.6 %gather_fusion = f32[512,384]{1,0:T(8,128)S(1)} fusion(f32[512,384]{1,0:T(8,128)S(1)} %fusion, s32[1024]{0:T(1024)S(1)} %pad_clamp_fusion), kind=kCustom, calls=%fused_computation | custom fusion | bytes 1574912 | tf_op jit(solution)/shard_map/jit(_take)/gather | solution.py:62
  121.4 0.0 copy-start.4
  121.5 0.0 copy-start.5
  121.5 0.1 broadcast_select_fusion
  121.6 0.2 multiply_reduce_fusion.1
  121.8 0.3 copy-done.4
  122.1 0.0 copy-done.5
  122.1 0.4 fusion.31
  122.5 0.2 fusion.10
  122.8 0.5 convolution_convert_fusion.1
  123.3 7.4 %all_to_all.16 = bf16[4,128,128]{2,1,0:T(8,128)(2,1)S(1)} all-to-all(bf16[4,128,128]{2,1,0:T(8,128)(2,1)S(1)} %bitcast.33), channel_id=1, replica_groups=mesh['sec'=2,'tp'=4,'dp'=4] {'tp'}, dimensions={0} | all-to-all | bytes 262144 | tf_op jit(solution)/shard_map/all_to_all | solution.py:124
  130.7 0.1 copy.15
  130.8 0.7 broadcast_in_dim.132
  (18 shorter events, 0.1 us)
Async XLA Ops:
  0.0 116.0 %copy-start = (bf16[192,3072]{1,0:T(8,128)(2,1)S(1)}, bf16[192,3072]{1,0:T(8,128)(2,1)}, u32[]{:S(2)}) copy-start(bf16[192,3072]{1,0:T(8,128)(2,1)} %param.14) | copy-start | bytes 3538948
  0.0 47.0 %copy-start.2 = (bf16[384,128]{1,0:T(8,128)(2,1)S(1)}, bf16[384,128]{1,0:T(8,128)(2,1)}, u32[]{:S(2)}) copy-start(bf16[384,128]{1,0:T(8,128)(2,1)} %param.17) | copy-start | bytes 294916
  0.0 92.3 %collective-permute-start.1 = (bf16[384,128]{1,0:T(8,128)(2,1)}, bf16[384,128]{1,0:T(8,128)(2,1)S(1)}, u32[]{:S(2)}, u32[]{:S(2)}) collective-permute-start(bf16[384,128]{1,0:T(8,128)(2,1)} %param.16), channel_id=1, source_target_pairs={{0,1},{1,2},{2,3},{3,16},{16,17},{17,18},{18,19},{19,0},{4,5},{5,6... | collective-permute-start | bytes 294920 | tf_op jit(solution)/shard_map/ppermute | solution.py:21
  3.1 89.2 %collective-permute-start.2 = (bf16[384,128]{1,0:T(8,128)(2,1)}, bf16[384,128]{1,0:T(8,128)(2,1)S(1)}, u32[]{:S(2)}, u32[]{:S(2)}) collective-permute-start(bf16[384,128]{1,0:T(8,128)(2,1)} %param.16), channel_id=1, source_target_pairs={{0,19},{1,0},{2,1},{3,2},{16,3},{17,16},{18,17},{19,18},{4,23},{5,... | collective-permute-start | bytes 294920 | tf_op jit(solution)/shard_map/ppermute | solution.py:26
  6.9 75.5 %collective-permute-start = (bf16[32,512]{1,0:T(8,128)(2,1)S(1)}, bf16[32,512]{1,0:T(8,128)(2,1)S(1)}, u32[]{:S(2)}, u32[]{:S(2)}) collective-permute-start(bf16[32,512]{1,0:T(8,128)(2,1)S(1)} %slice_bitcast_fusion), channel_id=1, source_target_pairs={{0,4},{4,8},{8,12},{1,5},{5,9},{9,13},{2,6},{6,10},{10,14},{3,7},{... | collective-permute-start | bytes 98312 | tf_op jit(solution)/shard_map/ppermute | solution.py:36
  12.8 68.5 %copy-start.3 = (bf16[384,128]{1,0:T(8,128)(2,1)S(1)}, bf16[384,128]{1,0:T(8,128)(2,1)}, u32[]{:S(2)}) copy-start(bf16[384,128]{1,0:T(8,128)(2,1)} %param.16) | copy-start | bytes 294916
  47.0 35.4 %copy-start.1 = (bf16[1,128,512]{2,1,0:T(8,128)(2,1)S(1)}, bf16[1,128,512]{2,1,0:T(8,128)(2,1)}, u32[]{:S(2)}) copy-start(bf16[1,128,512]{2,1,0:T(8,128)(2,1)} %param.10) | copy-start | bytes 393220
  92.3 8.4 %collective-permute-start.3 = (bf16[384,128]{1,0:T(8,128)(2,1)S(1)}, bf16[384,128]{1,0:T(8,128)(2,1)S(1)}, u32[]{:S(2)}, u32[]{:S(2)}) collective-permute-start(bf16[384,128]{1,0:T(8,128)(2,1)S(1)} %collective-permute-done.1), channel_id=1, source_target_pairs={{0,1},{1,2},{2,3},{3,16},{16,17},{17,18},{18,19},{19,0},{4,5},{5,6... | collective-permute-start | bytes 294920 | tf_op jit(solution)/shard_map/ppermute | solution.py:21
  92.3 8.4 %collective-permute-start.4 = (bf16[384,128]{1,0:T(8,128)(2,1)S(1)}, bf16[384,128]{1,0:T(8,128)(2,1)S(1)}, u32[]{:S(2)}, u32[]{:S(2)}) collective-permute-start(bf16[384,128]{1,0:T(8,128)(2,1)S(1)} %collective-permute-done.2), channel_id=1, source_target_pairs={{0,19},{1,0},{2,1},{3,2},{16,3},{17,16},{18,17},{19,18},{4,23},{5,... | collective-permute-start | bytes 294920 | tf_op jit(solution)/shard_map/ppermute | solution.py:26
  100.7 7.4 %collective-permute-start.5 = (bf16[384,128]{1,0:T(8,128)(2,1)S(1)}, bf16[384,128]{1,0:T(8,128)(2,1)S(1)}, u32[]{:S(2)}, u32[]{:S(2)}) collective-permute-start(bf16[384,128]{1,0:T(8,128)(2,1)S(1)} %collective-permute-done.3), channel_id=1, source_target_pairs={{0,1},{1,2},{2,3},{3,16},{16,17},{17,18},{18,19},{19,0},{4,5},{5,6... | collective-permute-start | bytes 294920 | tf_op jit(solution)/shard_map/ppermute | solution.py:21
  100.7 8.0 %collective-permute-start.6 = (bf16[384,128]{1,0:T(8,128)(2,1)S(1)}, bf16[384,128]{1,0:T(8,128)(2,1)S(1)}, u32[]{:S(2)}, u32[]{:S(2)}) collective-permute-start(bf16[384,128]{1,0:T(8,128)(2,1)S(1)} %collective-permute-done.4), channel_id=1, source_target_pairs={{0,19},{1,0},{2,1},{3,2},{16,3},{17,16},{18,17},{19,18},{4,23},{5,... | collective-permute-start | bytes 294920 | tf_op jit(solution)/shard_map/ppermute | solution.py:26
  108.1 7.3 %collective-permute-start.7 = (bf16[384,128]{1,0:T(8,128)(2,1)S(1)}, bf16[384,128]{1,0:T(8,128)(2,1)S(1)}, u32[]{:S(2)}, u32[]{:S(2)}) collective-permute-start(bf16[384,128]{1,0:T(8,128)(2,1)S(1)} %collective-permute-done.5), channel_id=1, source_target_pairs={{0,1},{1,2},{2,3},{3,16},{16,17},{17,18},{18,19},{19,0},{4,5},{5,6... | collective-permute-start | bytes 294920 | tf_op jit(solution)/shard_map/ppermute | solution.py:21
  121.4 0.7 copy-start.4
  121.5 0.7 copy-start.5
